TPU v7x, 32 devices: a whole 2x2x4 slice. The times are simulated.
32 devices in a mesh: row: 8 (over y, x, core), col: 4 (over z).
Axes of the slice: x: 2, y: 2, z: 4, core: 2. Of those that a mesh axis runs over, the one named last changes fastest.
Arguments:
- object_field: float32 [2, 3072, 1536], P(None, 'row', 'col'), may hold values from -4 to 4
- illumination: float32 [2, 256, 256], replicated, may hold values from -4 to 4
- measured: float32 [8, 4, 8, 256, 256], P('row', 'col'), may hold values from 0.05 to 4
- positions: int32 [8, 4, 8, 2], P('row', 'col'), may hold values from 0 to 383
- frame_counts: int32 [8, 4], P('row', 'col'), may hold values from 1 to 8, as said below
- first_count: int32 [8, 4], P('row', 'col'), may hold values from 0 to 4
Outputs:
- new_object: float32 [2, 3072, 1536], P(None, 'row', 'col')
- new_illumination: float32 [2, 256, 256], replicated
Inputs may be any that keep to these rules, and one draw needn't show every extreme that they name: `frame_counts`: some tile has exactly 8 live frames in every draw; slots from a tile's count on are unused.
All inputs are finite; a program needn't handle non-finite values.
Results may differ from a plain program's by a relative error of at most 0.0003.
Values sent between devices are 32-bit elements; how exact they have to be, the bound alone decides.
No kernel may reach another device: no remote copies, remote signals or barrier semaphores. Data moves between devices by JAX's collectives and lax.ppermute only.
A program may use at most 64 MiB of HBM per device.

v0:
```python
import math

import jax
import jax.numpy as jnp
import numpy as np
from jax import lax
from jax.experimental import pallas as pl
from jax.experimental.pallas import tpu as pltpu
from jax.sharding import PartitionSpec as P


LANES = 128


def shift(value, axis, steps):
    count = lax.axis_size(axis)
    leading, last = (max(0, -steps), min(count, count - steps))
    return lax.ppermute(value, axis, [(source, source + steps) for source in range(leading, last)])


def split(value):
    high = value.astype(jnp.bfloat16)
    low = (value - high.astype(jnp.float32)).astype(jnp.bfloat16)
    return high, low


def half_tables(length):
    half = length // 2
    m = np.arange(half)[:, None]
    n = np.arange(half)[None, :]
    tables = []
    for odd in (0, 1):
        angle = ((2 * m + odd) * n % length) * (2.0 * math.pi / length)
        c, s = np.cos(angle) / math.sqrt(length), np.sin(angle) / math.sqrt(length)
        real = np.block([[c, s], [-s, c]])
        tables += [real, real.T]
    stacked = np.stack(tables)
    high = stacked.astype(jnp.bfloat16)
    low = (stacked - high.astype(np.float64)).astype(jnp.bfloat16)
    return jnp.asarray(np.concatenate([high, low]))


def sorter(length):
    half = length // 2
    rows = np.arange(length)
    source = np.where(rows < half, 2 * rows, 2 * (rows - half) + 1)
    return jnp.asarray(np.eye(length)[source].astype(jnp.bfloat16))


def dot(left, right):
    return jnp.dot(left, right, preferred_element_type=jnp.float32)


def sort_kernel(count_ref, sorter_ref, unsorter_ref, in_ref, out_ref):
    def three(value):
        high, mid = split(value)
        low = (value - high.astype(jnp.float32) - mid.astype(jnp.float32)).astype(jnp.bfloat16)
        return high, mid, low

    def frame(slot, carry):
        high, mid, low = three(in_ref[slot])
        columns = dot(high, unsorter_ref[...]) + dot(mid, unsorter_ref[...]) + dot(low, unsorter_ref[...])
        high, mid, low = three(columns)
        out_ref[slot] = dot(sorter_ref[...], high) + dot(sorter_ref[...], mid) + dot(sorter_ref[...], low)
        return carry

    lax.fori_loop(0, count_ref[0, 0], frame, 0)


def frame_loop(start, stop, pos_ref, tab_ref, probe_ref, sorted_ref, ext, grad, gprobe_ref, win, pro):
    length = probe_ref.shape[1]
    half = length // 2
    me, met, mo, mot, le, let, lo, lot = (tab_ref.at[i] for i in range(8))

    def left(high_table, low_table, high, low):
        return dot(high_table[...], high) + dot(high_table[...], low) + dot(low_table[...], high)

    def right(high, low, high_table, low_table):
        return dot(high, high_table[...]) + dot(low, high_table[...]) + dot(high, low_table[...])

    def pair(step, carry):
        first_slot = start + 2 * step
        second_slot = jnp.minimum(first_slot + 1, stop - 1)
        slots = (first_slot, second_slot)
        alive = jnp.where(first_slot + 1 < stop, 1.0, 0.0)
        both = (0, 1)
        lane = lax.broadcasted_iota(jnp.int32, (length, LANES), 1)
        row = [pos_ref[s, 0] for s in slots]
        tile = [lax.shift_right_logical(pos_ref[s, 1], 7) for s in slots]
        turn = [lax.bitwise_and(pos_ref[s, 1], LANES - 1) for s in slots]

        def enter(f):
            first = lane >= turn[f]
            rows = pl.ds(row[f], length)
            for p in range(2):
                a = pltpu.roll(probe_ref[p, :, :LANES], turn[f], 1)
                b = pltpu.roll(probe_ref[p, :, LANES:], turn[f], 1)
                pro[f, p, :, :LANES] = jnp.where(first, a, b)
                pro[f, p, :, LANES:] = jnp.where(first, b, a)
                win[f, p, :, :LANES] = jnp.where(first, ext[p, tile[f], rows, :], ext[p, tile[f] + 2, rows, :])
                win[f, p, :, LANES:] = ext[p, tile[f] + 1, rows, :]

            def leave(at):
                pr, pi, wr, wi = (pro[f, 0, at, :], pro[f, 1, at, :], win[f, 0, at, :], win[f, 1, at, :])
                return pr * wr - pi * wi, pr * wi + pi * wr

            tr, ti = leave(pl.ds(0, half))
            br, bi = leave(pl.ds(half, half))
            uh, ul = split(jnp.concatenate([tr + br, ti + bi], axis=0))
            vh, vl = split(jnp.concatenate([tr - br, ti - bi], axis=0))
            return uh, ul, vh, vl

        def fold(block):
            r, i = block[:half], block[half:]
            ra, rb, ia, ib = (r[:, :LANES], r[:, LANES:], i[:, :LANES], i[:, LANES:])
            return (
                jnp.concatenate([ra + rb, ia + ib], axis=1),
                jnp.concatenate([ra - rb, ia - ib], axis=1),
            )

        def weigh(wave, target, f):
            r, i = wave[:, :LANES], wave[:, LANES:]
            residue = r * r + i * i - target
            if f:
                residue = residue * alive
            return split(jnp.concatenate([residue * r, residue * i], axis=1))

        def middle(even, odd, f):
            eu, ev = fold(even)
            ou, ov = fold(odd)
            uh, ul = split(jnp.concatenate([eu, ou], axis=0))
            vh, vl = split(jnp.concatenate([ev, ov], axis=0))
            wave_even = right(uh, ul, met, let)
            wave_odd = right(vh, vl, mot, lot)
            eh, el = weigh(wave_even, sorted_ref[slots[f], :, :LANES], f)
            oh, ol = weigh(wave_odd, sorted_ref[slots[f], :, LANES:], f)
            e = right(eh, el, me, le)
            o = right(oh, ol, mo, lo)
            near, far = e + o, e - o

            def rejoin(at):
                return split(
                    jnp.concatenate(
                        [
                            jnp.concatenate([near[at, :LANES], far[at, :LANES]], axis=1),
                            jnp.concatenate([near[at, LANES:], far[at, LANES:]], axis=1),
                        ],
                        axis=0,
                    )
                )

            return rejoin(slice(0, half)) + rejoin(slice(half, length))

        def exit_terms(f, e, o):
            mask = lane[:half] >= turn[f]
            unturn = lax.bitwise_and(LANES - turn[f], LANES - 1)
            keep = lane[:half] < LANES - turn[f]
            for back, at in ((e + o, 0), (e - o, half)):
                gr, gi = back[:half], back[half:]
                chunk = pl.ds(at, half)
                pr, pi = pro[f, 0, chunk, :], pro[f, 1, chunk, :]
                wr, wi = win[f, 0, chunk, :], win[f, 1, chunk, :]
                here = pl.ds(row[f] + at, half)
                for p, term in ((0, wr * gr + wi * gi), (1, wr * gi - wi * gr)):
                    a, b = pltpu.roll(term[:, :LANES], unturn, 1), pltpu.roll(term[:, LANES:], unturn, 1)
                    gprobe_ref[p, chunk, :LANES] = gprobe_ref[p, chunk, :LANES] + jnp.where(keep, a, b)
                    gprobe_ref[p, chunk, LANES:] = gprobe_ref[p, chunk, LANES:] + jnp.where(keep, b, a)
                for p, term in ((0, pr * gr + pi * gi), (1, pr * gi - pi * gr)):
                    side, mid = term[:, :LANES], term[:, LANES:]
                    grad[p, tile[f], here, :] = grad[p, tile[f], here, :] + jnp.where(mask, side, 0.0)
                    grad[p, tile[f] + 1, here, :] = grad[p, tile[f] + 1, here, :] + mid
                    grad[p, tile[f] + 2, here, :] = grad[p, tile[f] + 2, here, :] + jnp.where(mask, 0.0, side)

        entered = [enter(f) for f in both]
        halves = [(left(me, le, uh, ul), left(mo, lo, vh, vl)) for uh, ul, vh, vl in entered]
        joined = [middle(even, odd, f) for f, (even, odd) in zip(both, halves)]
        ends = [(left(met, let, eh, el), left(mot, lot, oh, ol)) for eh, el, oh, ol in joined]
        for f, (e, o) in zip(both, ends):
            exit_terms(f, e, o)
        return carry

    lax.fori_loop(0, lax.shift_right_logical(stop - start + 1, 1), pair, 0)


def seat_order(value_ref, core, seat, members, out_ref):
    height = out_ref.shape[0] // members
    for j in range(members):
        rows = pl.ds(pl.multiple_of(lax.bitwise_xor(seat, j) * height, height), height)
        out_ref[j * height : (j + 1) * height, :] = value_ref[core, rows, :]


def put(ext, piece, row, col):
    for p in range(2):
        for j in range(piece.shape[2] // LANES):
            ext[p, col // LANES + j, row : row + piece.shape[1], :] = piece[p, :, j * LANES : (j + 1) * LANES]


def first_kernel(*refs):
    count_ref, first_ref, pos_ref, tab_ref, probe_ref, sorted_ref = refs[:6]
    own, right_top, right_low, below, corner = refs[6:11]
    ext, grad, down0, up0, right1, left1, send_ref, keep_ref = refs[11:19]
    win, pro, gprobe_ref = refs[19:]
    n = probe_ref.shape[1]
    tile = own.shape[1]
    put(ext, own, 0, 0)
    put(ext, right_top, 0, tile)
    put(ext, right_low, n, tile)
    put(ext, below, tile, 0)
    put(ext, corner, tile, tile)
    grad[...] = jnp.zeros_like(grad)
    gprobe_ref[...] = jnp.zeros_like(gprobe_ref)
    stop = jnp.minimum(first_ref[0, 0], count_ref[0, 0])
    frame_loop(0, stop, pos_ref, tab_ref, probe_ref, sorted_ref, ext, grad, gprobe_ref, win, pro)
    core, seat = row_bits()
    members = lax.axis_size("row") // 2
    seat_order(gprobe_ref, 1 - core, seat, members, send_ref)
    seat_order(gprobe_ref, core, seat, members, keep_ref)
    t = tile // LANES
    down0[...] = grad[0, :, tile:, :]
    up0[...] = grad[0, :, :n, :]
    right1[...] = grad[1, t:, :, :]
    left1[...] = grad[1, : n // LANES, :, :]


def columns_kernel(grad, above, below, right0, left0):
    n, side = above.shape[1], grad.shape[2]
    t, w = grad.shape[1] - n // LANES, n // LANES
    for out, at in ((right0, slice(t, t + w)), (left0, slice(0, w))):
        out[:, :n, :] = grad[0, at, :n, :] + above[at]
        out[:, n : side - n, :] = grad[0, at, n : side - n, :]
        out[:, side - n :, :] = grad[0, at, side - n :, :] + below[at]


def rows_kernel(grad, before, after, down1, up1):
    w = before.shape[0]
    tiles, side = grad.shape[1], grad.shape[2]
    n = down1.shape[1]
    for out, at in ((down1, slice(side - n, side)), (up1, slice(0, n))):
        out[:w] = grad[1, :w, at, :] + before[:, at, :]
        out[w : tiles - w] = grad[1, w : tiles - w, at, :]
        out[tiles - w :] = grad[1, tiles - w :, at, :] + after[:, at, :]


def second_kernel(step_size, *refs):
    count_ref, first_ref, pos_ref, tab_ref, probe_ref, sorted_ref = refs[:6]
    old, g1, above0, below0, before0, after0, before1, after1, above1, below1, plane, other = refs[6:18]
    grad, new_ref, new_probe, down_r, down_l, low_r, send_ref, keep_ref = refs[18:26]
    ext, win, pro, gprobe_ref = refs[26:]
    n, side, tiles = probe_ref.shape[1], ext.shape[2], ext.shape[1]
    tile, w = side - n, n // LANES
    t = tile // LANES
    step_probe(probe_ref, plane, other, new_probe, step_size)
    inside_col = jnp.where(lax.axis_index("col") < lax.axis_size("col") - 1, 0.1, 0.0)
    inside_row = jnp.where(lax.axis_index("row") < lax.axis_size("row") - 1, 1.0, 0.0)
    for p, (above, below, before, after) in enumerate(
        ((above0, below0, before0, after0), (above1, below1, before1, after1))
    ):
        for j in range(tiles):
            weight = 0.1 if j < t else inside_col
            for r0, r1, side_rows in ((0, n, above), (n, tile, None), (tile, side, below)):
                total = g1[p, j, r0:r1, :]
                if side_rows is not None:
                    total = total + side_rows[j]
                if j < w:
                    total = total + before[j, r0:r1, :]
                if j >= t:
                    total = total + after[j - t, r0:r1, :]
                scale = weight * inside_row if r0 == tile else weight
                ext[p, j, r0:r1, :] = old[p, j, r0:r1, :] - scale * total
    for p in range(2):
        for j in range(t):
            new_ref[p, :, j * LANES : (j + 1) * LANES] = ext[p, j, :tile, :]
    grad[...] = jnp.zeros_like(grad)
    gprobe_ref[...] = jnp.zeros_like(gprobe_ref)
    stop = count_ref[0, 0]
    start = jnp.minimum(first_ref[0, 0], stop)
    frame_loop(start, stop, pos_ref, tab_ref, new_probe, sorted_ref, ext, grad, gprobe_ref, win, pro)
    core, seat = row_bits()
    members = lax.axis_size("row") // 2
    seat_order(gprobe_ref, 1 - core, seat, members, send_ref)
    seat_order(gprobe_ref, core, seat, members, keep_ref)
    down_r[...] = grad[:, t:, tile:, :]
    down_l[...] = grad[:, :t, tile:, :]
    low_r[...] = grad[:, t:, n:tile, :]


def join_kernel(grad, above, out):
    t, n = grad.shape[1] - above.shape[1], above.shape[2]
    out[...] = grad[:, t:, :n, :] + above[...]


def f32(*shape):
    return jax.ShapeDtypeStruct(shape, jnp.float32)


def vmem_call(kernel, out_shape, operands, scalars=(), scratch=(), limit=16):
    smem = [pl.BlockSpec(memory_space=pltpu.SMEM)] * len(scalars)
    vmem = pl.BlockSpec(memory_space=pltpu.VMEM)
    return pl.pallas_call(
        kernel,
        in_specs=smem + [vmem] * len(operands),
        out_specs=jax.tree.map(lambda _: vmem, out_shape),
        out_shape=out_shape,
        scratch_shapes=list(scratch),
        compiler_params=pltpu.CompilerParams(vmem_limit_bytes=limit * 1024 * 1024),
    )(*scalars, *operands)


def swap(value, axis, mask):
    count = lax.axis_size(axis)
    return lax.ppermute(value, axis, [(source, source ^ mask) for source in range(count)])


def row_bits():
    row = lax.axis_index("row")
    return lax.bitwise_and(row, 1), lax.shift_right_logical(row, 1)


def deal_kernel(keep_ref, heard_ref, *outs):
    height = outs[0].shape[0]
    for j, out in enumerate(outs):
        rows = slice(j * height, (j + 1) * height)
        out[...] = keep_ref[rows, :] + heard_ref[rows, :]


def steps_of(cols):
    steps = []
    step = 1
    while step < cols:
        steps.append(step)
        step *= 4
    return steps


def sum_probe(send, keep):
    members = lax.axis_size("row") // 2
    cols = lax.axis_size("col")
    height, width = keep.shape[0] // members, keep.shape[1]
    heard = swap(send, "row", 1)
    dealt = vmem_call(deal_kernel, [f32(height, width)] * members, (keep, heard))
    total = dealt[0]
    for value in [swap(dealt[j], "row", 2 * j) for j in range(1, members)]:
        total = total + value
    for step in steps_of(cols):
        near, *rest = [swap(total, "col", m * step) for m in (1, 2, 3) if m * step < cols]
        total = total + near
        if rest:
            total = total + (rest[0] + rest[1])
    parts = [total] + [swap(total, "row", 2 * j) for j in range(1, members)]
    plane = jnp.concatenate(parts, axis=0)
    return plane, swap(plane, "row", 1)


def step_probe(old_ref, plane_ref, other_ref, new_ref, step_size):
    core, seat = row_bits()
    members = lax.axis_size("row") // 2
    height = plane_ref.shape[0] // members
    for j in range(members):
        rows = pl.ds(pl.multiple_of(lax.bitwise_xor(seat, j) * height, height), height)
        here = slice(j * height, (j + 1) * height)
        new_ref[core, rows, :] = old_ref[core, rows, :] - step_size * plane_ref[here, :]
        new_ref[1 - core, rows, :] = old_ref[1 - core, rows, :] - step_size * other_ref[here, :]


def finish_kernel(old_ref, grad, above, before_top, before_low, out_ref):
    n, w = above.shape[2], before_top.shape[1]
    tile = out_ref.shape[1]
    for p in range(2):
        for j in range(tile // LANES):
            here = slice(j * LANES, (j + 1) * LANES)
            top = grad[p, j, :n, :] + above[p, j]
            low = grad[p, j, n:tile, :]
            if j < w:
                top = top + before_top[p, j]
                low = low + before_low[p, j]
            out_ref[p, :n, here] = old_ref[p, :n, here] - 0.1 * top
            out_ref[p, n:, here] = old_ref[p, n:, here] - 0.1 * low


def per_device(object_field, illumination, measured, positions, frame_counts, first_count):
    n = illumination.shape[1]
    tile = object_field.shape[1]
    side = tile + n
    tiles, w, t = side // LANES, n // LANES, tile // LANES
    devices = lax.axis_size("row") * lax.axis_size("col")
    step_size = 0.5 / math.sqrt(devices * measured.shape[2])
    tables = half_tables(n)
    scalars = (frame_counts, first_count, positions[0, 0])
    o = object_field

    right_top = shift(o[:, :n, :n], "col", -1)
    right_low = shift(o[:, n:, :n], "col", -1)
    below = shift(o[:, :n, :], "row", -1)
    order = sorter(n)
    sorted_measured = vmem_call(
        sort_kernel, f32(*measured.shape[2:]), (order, order.T, measured[0, 0]), (frame_counts,)
    )
    right_top, sorted_measured = lax.optimization_barrier((right_top, sorted_measured))
    corner = shift(right_top, "row", -1)

    work = [pltpu.VMEM((2,) + illumination.shape, jnp.float32)] * 2 + [pltpu.VMEM(illumination.shape, jnp.float32)]
    whole, plane_shape = f32(2, tiles, side, LANES), f32(n, n)
    row_strip, col_strip = f32(tiles, n, LANES), f32(w, side, LANES)
    ext, grad, down0, up0, right1, left1, send, keep = vmem_call(
        first_kernel,
        [whole, whole, row_strip, row_strip, col_strip, col_strip, plane_shape, plane_shape],
        (tables, illumination, sorted_measured, o, right_top, right_low, below, corner),
        scalars,
        work,
        28,
    )
    before1 = shift(right1, "col", 1)
    after1 = shift(left1, "col", -1)
    above0 = shift(down0, "row", 1)
    below0 = shift(up0, "row", -1)
    right0, left0 = vmem_call(columns_kernel, [col_strip] * 2, (grad, above0, below0))
    before0 = shift(right0, "col", 1)
    after0 = shift(left0, "col", -1)
    down1, up1 = vmem_call(rows_kernel, [row_strip] * 2, (grad, before1, after1))
    above1 = shift(down1, "row", 1)
    below1 = shift(up1, "row", -1)
    plane, other = sum_probe(send, keep)

    grad, new_object, new_probe, down_r, down_l, low_r, send, keep = vmem_call(
        lambda *refs: second_kernel(step_size, *refs),
        [whole, f32(*o.shape), f32(*illumination.shape), f32(2, w, n, LANES), f32(2, t, n, LANES),
         f32(2, w, tile - n, LANES), plane_shape, plane_shape],
        (tables, illumination, sorted_measured, ext, grad, above0, below0, before0, after0,
         before1, after1, above1, below1, plane, other),
        scalars,
        [pltpu.VMEM(whole.shape, jnp.float32)] + work,
        28,
    )
    above_r = shift(down_r, "row", 1)
    before_low = shift(low_r, "col", 1)
    above_l = shift(down_l, "row", 1)
    joined = vmem_call(join_kernel, f32(*above_r.shape), (grad, above_r))
    before_top = shift(joined, "col", 1)
    new_object = vmem_call(finish_kernel, f32(*o.shape), (new_object, grad, above_l, before_top, before_low))
    plane, other = sum_probe(send, keep)
    new_probe = vmem_call(
        lambda *refs: step_probe(*refs, step_size), f32(*illumination.shape), (new_probe, plane, other)
    )
    return (new_object, new_probe)


def solution(mesh):
    in_specs = (
        P(None, "row", "col"),
        P(),
        P("row", "col", None, None, None),
        P("row", "col", None, None),
        P("row", "col"),
        P("row", "col"),
    )
    out_specs = (P(None, "row", "col"), P())
    return jax.shard_map(per_device, mesh=mesh, in_specs=in_specs, out_specs=out_specs, check_vma=False)
```

profile of v0, /device:TPU:0, one launch (start us, length us, event | category | flops | bytes accessed | tf_op | source)
XLA Modules:
  0.0 165.0 jit_solution(1117839283073224127)
XLA Ops:
  3.2 2.1 %slice.11 = f32[2,256,384]{2,1,0:T(8,128)} slice(f32[2,384,384]{2,1,0:T(8,128)} %refs_6_.1), slice={[0:2], [0:256], [0:384]} | slice | bytes 1572864 | tf_op jit(solution)/shard_map/slice | solution.py:393
  7.3 5.4 %shard_map.95.refs_5_ = f32[8,256,256]{2,1,0:T(8,128)S(1)} custom-call(s32[1,1]{1,0:T(1,128)S(6)} %copy.12.count_ref.refs_0_, bf16[256,256]{1,0:T(8,128)(2,1)S(1)} %copy-done.5, bf16[256,256]{1,0:T(8,128)(2,1)S(1)} %copy-done.4, f32[8,256,256]{2,1,0:T(8,128)S(1)} %bitcast.2), custom_call_target="tpu_custom_call" | custom-call | tf_op jit(solution)/shard_map/pallas_call | solution.py:299
  12.7 6.2 %collective-permute-done.refs_7_ = f32[2,256,256]{2,1,0:T(8,128)} collective-permute-done((f32[2,256,256]{2,1,0:T(8,128)S(1)}, f32[2,256,256]{2,1,0:T(8,128)}, u32[]{:S(2)}, u32[]{:S(2)}) %collective-permute-start) | collective-permute-done | bytes 524320 | tf_op jit(solution)/shard_map/ppermute | solution.py:18
  22.9 9.1 %collective-permute-done.1.refs_8_ = f32[2,128,256]{2,1,0:T(8,128)S(1)} collective-permute-done((f32[2,128,256]{2,1,0:T(8,128)}, f32[2,128,256]{2,1,0:T(8,128)S(1)}, u32[]{:S(2)}, u32[]{:S(2)}) %collective-permute-start.1) | collective-permute-done | bytes 262176 | tf_op jit(solution)/shard_map/ppermute | solution.py:18
  34.3 5.1 %shard_map.96 = (f32[2,5,640,128]{3,2,1,0:T(8,128)S(1)}, f32[2,5,640,128]{3,2,1,0:T(8,128)S(1)}, f32[5,256,128]{2,1,0:T(8,128)S(1)}, f32[5,256,128]{2,1,0:T(8,12...) custom-call(s32[1,1]{1,0:T(1,128)S(6)} %copy.12.count_ref.refs_0_, ...), custom_call_target="tpu_custom_call" | custom-call | tf_op jit(solution)/shard_map/pallas_call | solution.py:299
  39.6 6.5 %collective-permute-start.8 = (f32[2,640,128]{2,1,0:T(8,128)S(1)}, f32[2,640,128]{2,1,0:T(8,128)S(1)}, u32[]{:S(2)}, u32[]{:S(2)}) collective-permute-start(f32[2,640,128]{2,1,0:T(8,128)S(1)} %get-tuple-element.40), channel_id=1, source_target_pairs={{0,1},{1,2},{2,3},{4,5},{5,6},{6,7},{8,9},{9,10},{10,11},{12,13},{... | collective-permute-start | bytes 1966088 | tf_op jit(solution)/shard_map/ppermute | solution.py:18
  47.3 2.1 %collective-permute-start.4 = (f32[5,256,128]{2,1,0:T(8,128)S(1)}, f32[5,256,128]{2,1,0:T(8,128)S(1)}, u32[]{:S(2)}, u32[]{:S(2)}) collective-permute-start(f32[5,256,128]{2,1,0:T(8,128)S(1)} %get-tuple-element.36), channel_id=1, source_target_pairs={{0,4},{4,8},{8,12},{12,16},{16,20},{20,24},{24,28},{1,5},{5,9},{9,... | collective-permute-start | bytes 1966088 | tf_op jit(solution)/shard_map/ppermute | solution.py:18
  50.8 4.1 %collective-permute-start.13 = (f32[64,256]{1,0:T(8,128)S(1)}, f32[64,256]{1,0:T(8,128)S(1)}, u32[]{:S(2)}, u32[]{:S(2)}) collective-permute-start(f32[64,256]{1,0:T(8,128)S(1)} %get-tuple-element.47), channel_id=1, source_target_pairs={{0,8},{4,12},{8,0},{12,4},{16,24},{20,28},{24,16},{28,20},{1,9},{5... | collective-permute-start | bytes 196616 | tf_op jit(solution)/shard_map/ppermute | solution.py:311
  55.0 12.7 %collective-permute-done.13 = f32[64,256]{1,0:T(8,128)S(1)} collective-permute-done((f32[64,256]{1,0:T(8,128)S(1)}, f32[64,256]{1,0:T(8,128)S(1)}, u32[]{:S(2)}, u32[]{:S(2)}) %collective-permute-start.13) | collective-permute-done | bytes 65568 | tf_op jit(solution)/shard_map/ppermute | solution.py:311
  67.7 4.3 %collective-permute-done.14 = f32[64,256]{1,0:T(8,128)S(1)} collective-permute-done((f32[64,256]{1,0:T(8,128)S(1)}, f32[64,256]{1,0:T(8,128)S(1)}, u32[]{:S(2)}, u32[]{:S(2)}) %collective-permute-start.14) | collective-permute-done | bytes 65568 | tf_op jit(solution)/shard_map/ppermute | solution.py:311
  72.1 5.0 %collective-permute-done.15 = f32[64,256]{1,0:T(8,128)S(1)} collective-permute-done((f32[64,256]{1,0:T(8,128)S(1)}, f32[64,256]{1,0:T(8,128)S(1)}, u32[]{:S(2)}, u32[]{:S(2)}) %collective-permute-start.15) | collective-permute-done | bytes 65568 | tf_op jit(solution)/shard_map/ppermute | solution.py:311
  77.1 4.3 %collective-permute-start.18 = (f32[64,256]{1,0:T(8,128)S(1)}, f32[64,256]{1,0:T(8,128)S(1)}, u32[]{:S(2)}, u32[]{:S(2)}) collective-permute-start(f32[64,256]{1,0:T(8,128)S(1)} %add_add_fusion.3), channel_id=1, source_target_pairs={{0,3},{1,2},{2,1},{3,0},{4,7},{5,6},{6,5},{7,4},{8,11},{9,10},{10,... | collective-permute-start | bytes 196616 | tf_op jit(solution)/shard_map/ppermute | solution.py:311
  85.1 3.6 %collective-permute-start.6 = (f32[2,640,128]{2,1,0:T(8,128)S(1)}, f32[2,640,128]{2,1,0:T(8,128)S(1)}, u32[]{:S(2)}, u32[]{:S(2)}) collective-permute-start(f32[2,640,128]{2,1,0:T(8,128)S(1)} %get-tuple-element.38), channel_id=1, source_target_pairs={{0,1},{1,2},{2,3},{4,5},{5,6},{6,7},{8,9},{9,10},{10,11},{12,13},{... | collective-permute-start | bytes 1966088 | tf_op jit(solution)/shard_map/ppermute | solution.py:18
  90.0 5.8 %collective-permute-start.21 = (f32[64,256]{1,0:T(8,128)S(1)}, f32[64,256]{1,0:T(8,128)S(1)}, u32[]{:S(2)}, u32[]{:S(2)}) collective-permute-start(f32[64,256]{1,0:T(8,128)S(1)} %add_add_fusion.2), channel_id=1, source_target_pairs={{0,24},{4,28},{8,16},{12,20},{16,8},{20,12},{24,0},{28,4},{1,25},{... | collective-permute-start | bytes 196616 | tf_op jit(solution)/shard_map/ppermute | solution.py:311
  95.7 4.5 %collective-permute-done.21 = f32[64,256]{1,0:T(8,128)S(1)} collective-permute-done((f32[64,256]{1,0:T(8,128)S(1)}, f32[64,256]{1,0:T(8,128)S(1)}, u32[]{:S(2)}, u32[]{:S(2)}) %collective-permute-start.21) | collective-permute-done | bytes 65568 | tf_op jit(solution)/shard_map/ppermute | solution.py:311
  100.3 3.8 %collective-permute-start.20 = (f32[64,256]{1,0:T(8,128)S(1)}, f32[64,256]{1,0:T(8,128)S(1)}, u32[]{:S(2)}, u32[]{:S(2)}) collective-permute-start(f32[64,256]{1,0:T(8,128)S(1)} %add_add_fusion.2), channel_id=1, source_target_pairs={{0,16},{4,20},{8,24},{12,28},{16,0},{20,4},{24,8},{28,12},{1,17},{... | collective-permute-start | bytes 196616 | tf_op jit(solution)/shard_map/ppermute | solution.py:311
  104.1 2.2 %collective-permute-done.20 = f32[64,256]{1,0:T(8,128)S(1)} collective-permute-done((f32[64,256]{1,0:T(8,128)S(1)}, f32[64,256]{1,0:T(8,128)S(1)}, u32[]{:S(2)}, u32[]{:S(2)}) %collective-permute-start.20) | collective-permute-done | bytes 65568 | tf_op jit(solution)/shard_map/ppermute | solution.py:311
  106.4 3.0 %collective-permute-start.19 = (f32[64,256]{1,0:T(8,128)S(1)}, f32[64,256]{1,0:T(8,128)S(1)}, u32[]{:S(2)}, u32[]{:S(2)}) collective-permute-start(f32[64,256]{1,0:T(8,128)S(1)} %add_add_fusion.2), channel_id=1, source_target_pairs={{0,8},{4,12},{8,0},{12,4},{16,24},{20,28},{24,16},{28,20},{1,9},{5... | collective-permute-start | bytes 196616 | tf_op jit(solution)/shard_map/ppermute | solution.py:311
  109.4 2.2 %collective-permute-done.19 = f32[64,256]{1,0:T(8,128)S(1)} collective-permute-done((f32[64,256]{1,0:T(8,128)S(1)}, f32[64,256]{1,0:T(8,128)S(1)}, u32[]{:S(2)}, u32[]{:S(2)}) %collective-permute-start.19) | collective-permute-done | bytes 65568 | tf_op jit(solution)/shard_map/ppermute | solution.py:311
  111.7 1.5 collective-permute-done.22.refs_17_
  113.3 10.6 %shard_map.100 = (f32[2,5,640,128]{3,2,1,0:T(8,128)S(1)}, f32[2,384,384]{2,1,0:T(8,128)S(1)}, f32[2,256,256]{2,1,0:T(8,128)S(1)}, f32[2,2,256,128]{3,2,1,0:T(8,1...) custom-call(s32[1,1]{1,0:T(1,128)S(6)} %copy.12.count_ref.refs_0_, ...), custom_call_target="tpu_custom_call" | custom-call | tf_op jit(solution)/shard_map/pallas_call | solution.py:299
  124.0 2.4 %collective-permute-start.24 = (f32[2,2,256,128]{3,2,1,0:T(8,128)S(1)}, f32[2,2,256,128]{3,2,1,0:T(8,128)S(1)}, u32[]{:S(2)}, u32[]{:S(2)}) collective-permute-start(f32[2,2,256,128]{3,2,1,0:T(8,128)S(1)} %get-tuple-element.53), channel_id=1, source_target_pairs={{0,4},{4,8},{8,12},{12,16},{16,20},{20,24},{24,28},{1,5},{5,9},{9,... | collective-permute-start | bytes 1572872 | tf_op jit(solution)/shard_map/ppermute | solution.py:18
  126.5 4.6 %collective-permute-start.28 = (f32[64,256]{1,0:T(8,128)S(1)}, f32[64,256]{1,0:T(8,128)S(1)}, u32[]{:S(2)}, u32[]{:S(2)}) collective-permute-start(f32[64,256]{1,0:T(8,128)S(1)} %get-tuple-element.59), channel_id=1, source_target_pairs={{0,8},{4,12},{8,0},{12,4},{16,24},{20,28},{24,16},{28,20},{1,9},{5... | collective-permute-start | bytes 196616 | tf_op jit(solution)/shard_map/ppermute | solution.py:311
  131.1 1.5 collective-permute-start.30
  132.6 3.1 %collective-permute-start.23 = (f32[2,3,256,128]{3,2,1,0:T(8,128)S(1)}, f32[2,3,256,128]{3,2,1,0:T(8,128)S(1)}, u32[]{:S(2)}, u32[]{:S(2)}) collective-permute-start(f32[2,3,256,128]{3,2,1,0:T(8,128)S(1)} %get-tuple-element.52), channel_id=1, source_target_pairs={{0,4},{4,8},{8,12},{12,16},{16,20},{20,24},{24,28},{1,5},{5,9},{9,... | collective-permute-start | bytes 2359304 | tf_op jit(solution)/shard_map/ppermute | solution.py:18
  135.8 2.8 %collective-permute-done.29 = f32[64,256]{1,0:T(8,128)S(1)} collective-permute-done((f32[64,256]{1,0:T(8,128)S(1)}, f32[64,256]{1,0:T(8,128)S(1)}, u32[]{:S(2)}, u32[]{:S(2)}) %collective-permute-start.29) | collective-permute-done | bytes 65568 | tf_op jit(solution)/shard_map/ppermute | solution.py:311
  138.9 2.7 %collective-permute-start.32 = (f32[64,256]{1,0:T(8,128)S(1)}, f32[64,256]{1,0:T(8,128)S(1)}, u32[]{:S(2)}, u32[]{:S(2)}) collective-permute-start(f32[64,256]{1,0:T(8,128)S(1)} %add_add_fusion.1), channel_id=1, source_target_pairs={{0,2},{1,3},{2,0},{3,1},{4,6},{5,7},{6,4},{7,5},{8,10},{9,11},{10,... | collective-permute-start | bytes 196616 | tf_op jit(solution)/shard_map/ppermute | solution.py:311
  143.1 2.6 %collective-permute-start.25 = (f32[2,2,256,128]{3,2,1,0:T(8,128)S(1)}, f32[2,2,256,128]{3,2,1,0:T(8,128)S(1)}, u32[]{:S(2)}, u32[]{:S(2)}) collective-permute-start(f32[2,2,256,128]{3,2,1,0:T(8,128)S(1)} %shard_map.101), channel_id=1, source_target_pairs={{0,1},{1,2},{2,3},{4,5},{5,6},{6,7},{8,9},{9,10},{10,11},{12,13},{... | collective-permute-start | bytes 1572872 | tf_op jit(solution)/shard_map/ppermute | solution.py:18
  145.7 2.7 %collective-permute-done.32 = f32[64,256]{1,0:T(8,128)S(1)} collective-permute-done((f32[64,256]{1,0:T(8,128)S(1)}, f32[64,256]{1,0:T(8,128)S(1)}, u32[]{:S(2)}, u32[]{:S(2)}) %collective-permute-start.32) | collective-permute-done | bytes 65568 | tf_op jit(solution)/shard_map/ppermute | solution.py:311
  149.0 2.2 %collective-permute-start.35 = (f32[64,256]{1,0:T(8,128)S(1)}, f32[64,256]{1,0:T(8,128)S(1)}, u32[]{:S(2)}, u32[]{:S(2)}) collective-permute-start(f32[64,256]{1,0:T(8,128)S(1)} %add_add_fusion), channel_id=1, source_target_pairs={{0,16},{4,20},{8,24},{12,28},{16,0},{20,4},{24,8},{28,12},{1,17},{... | collective-permute-start | bytes 196616 | tf_op jit(solution)/shard_map/ppermute | solution.py:311
  151.2 1.4 collective-permute-start.34
  158.4 5.4 %collective-permute-done.26.before_low = f32[2,2,128,128]{3,2,1,0:T(8,128)S(1)} collective-permute-done((f32[2,2,128,128]{3,2,1,0:T(8,128)S(1)}, f32[2,2,128,128]{3,2,1,0:T(8,128)S(1)}, u32[]{:S(2)}, u32[]{:S(2)}) %collective-permute-start.26) | collective-permute-done | bytes 262176 | tf_op jit(solution)/shard_map/ppermute | solution.py:18
  (78 shorter events, 27.0 us)
Async XLA Ops:
  1.9 17.0 %collective-permute-start = (f32[2,256,256]{2,1,0:T(8,128)S(1)}, f32[2,256,256]{2,1,0:T(8,128)}, u32[]{:S(2)}, u32[]{:S(2)}) collective-permute-start(f32[2,256,256]{2,1,0:T(8,128)S(1)} %slice.9), channel_id=1, source_target_pairs={{1,0},{2,1},{3,2},{5,4},{6,5},{7,6},{9,8},{10,9},{11,10},{13,12},{... | collective-permute-start | bytes 1572872 | tf_op jit(solution)/shard_map/ppermute | solution.py:18
  5.3 26.8 %collective-permute-start.2 = (f32[2,256,384]{2,1,0:T(8,128)}, f32[2,256,384]{2,1,0:T(8,128)}, u32[]{:S(2)}, u32[]{:S(2)}) collective-permute-start(f32[2,256,384]{2,1,0:T(8,128)} %slice.11), channel_id=1, source_target_pairs={{4,0},{8,4},{12,8},{16,12},{20,16},{24,20},{28,24},{5,1},{9,5},{13... | collective-permute-start | bytes 2359304 | tf_op jit(solution)/shard_map/ppermute | solution.py:18
  18.9 13.1 %collective-permute-start.3 = (f32[2,256,256]{2,1,0:T(8,128)}, f32[2,256,256]{2,1,0:T(8,128)}, u32[]{:S(2)}, u32[]{:S(2)}) collective-permute-start(f32[2,256,256]{2,1,0:T(8,128)} %collective-permute-done.refs_7_), channel_id=1, source_target_pairs={{4,0},{8,4},{12,8},{16,12},{20,16},{24,20},{28,24},{5,1},{9,5},{13... | collective-permute-start | bytes 1572872 | tf_op jit(solution)/shard_map/ppermute | solution.py:18
  20.9 11.1 %collective-permute-start.1 = (f32[2,128,256]{2,1,0:T(8,128)}, f32[2,128,256]{2,1,0:T(8,128)S(1)}, u32[]{:S(2)}, u32[]{:S(2)}) collective-permute-start(f32[2,128,256]{2,1,0:T(8,128)} %slice.10), channel_id=1, source_target_pairs={{1,0},{2,1},{3,2},{5,4},{6,5},{7,6},{9,8},{10,9},{11,10},{13,12},{... | collective-permute-start | bytes 786440 | tf_op jit(solution)/shard_map/ppermute | solution.py:18
  39.4 11.4 %collective-permute-start.12 = (f32[256,256]{1,0:T(8,128)S(1)}, f32[256,256]{1,0:T(8,128)S(1)}, u32[]{:S(2)}, u32[]{:S(2)}) collective-permute-start(f32[256,256]{1,0:T(8,128)S(1)} %get-tuple-element.45), channel_id=1, source_target_pairs={{0,4},{4,0},{8,12},{12,8},{16,20},{20,16},{24,28},{28,24},{1,5},{5... | collective-permute-start | bytes 786440 | tf_op jit(solution)/shard_map/ppermute | solution.py:311
  39.6 41.9 %collective-permute-start.8 = (f32[2,640,128]{2,1,0:T(8,128)S(1)}, f32[2,640,128]{2,1,0:T(8,128)S(1)}, u32[]{:S(2)}, u32[]{:S(2)}) collective-permute-start(f32[2,640,128]{2,1,0:T(8,128)S(1)} %get-tuple-element.40), channel_id=1, source_target_pairs={{0,1},{1,2},{2,3},{4,5},{5,6},{6,7},{8,9},{9,10},{10,11},{12,13},{... | collective-permute-start | bytes 1966088 | tf_op jit(solution)/shard_map/ppermute | solution.py:18
  46.0 35.7 %collective-permute-start.9 = (f32[2,640,128]{2,1,0:T(8,128)S(1)}, f32[2,640,128]{2,1,0:T(8,128)S(1)}, u32[]{:S(2)}, u32[]{:S(2)}) collective-permute-start(f32[2,640,128]{2,1,0:T(8,128)S(1)} %get-tuple-element.41), channel_id=1, source_target_pairs={{1,0},{2,1},{3,2},{5,4},{6,5},{7,6},{9,8},{10,9},{11,10},{13,12},{... | collective-permute-start | bytes 1966088 | tf_op jit(solution)/shard_map/ppermute | solution.py:18
  47.3 34.9 %collective-permute-start.4 = (f32[5,256,128]{2,1,0:T(8,128)S(1)}, f32[5,256,128]{2,1,0:T(8,128)S(1)}, u32[]{:S(2)}, u32[]{:S(2)}) collective-permute-start(f32[5,256,128]{2,1,0:T(8,128)S(1)} %get-tuple-element.36), channel_id=1, source_target_pairs={{0,4},{4,8},{8,12},{12,16},{16,20},{20,24},{24,28},{1,5},{5,9},{9,... | collective-permute-start | bytes 1966088 | tf_op jit(solution)/shard_map/ppermute | solution.py:18
  49.5 34.1 %collective-permute-start.5 = (f32[5,256,128]{2,1,0:T(8,128)S(1)}, f32[5,256,128]{2,1,0:T(8,128)S(1)}, u32[]{:S(2)}, u32[]{:S(2)}) collective-permute-start(f32[5,256,128]{2,1,0:T(8,128)S(1)} %get-tuple-element.37), channel_id=1, source_target_pairs={{4,0},{8,4},{12,8},{16,12},{20,16},{24,20},{28,24},{5,1},{9,5},{13... | collective-permute-start | bytes 1966088 | tf_op jit(solution)/shard_map/ppermute | solution.py:18
  50.8 16.9 %collective-permute-start.13 = (f32[64,256]{1,0:T(8,128)S(1)}, f32[64,256]{1,0:T(8,128)S(1)}, u32[]{:S(2)}, u32[]{:S(2)}) collective-permute-start(f32[64,256]{1,0:T(8,128)S(1)} %get-tuple-element.47), channel_id=1, source_target_pairs={{0,8},{4,12},{8,0},{12,4},{16,24},{20,28},{24,16},{28,20},{1,9},{5... | collective-permute-start | bytes 196616 | tf_op jit(solution)/shard_map/ppermute | solution.py:311
  77.1 7.9 %collective-permute-start.18 = (f32[64,256]{1,0:T(8,128)S(1)}, f32[64,256]{1,0:T(8,128)S(1)}, u32[]{:S(2)}, u32[]{:S(2)}) collective-permute-start(f32[64,256]{1,0:T(8,128)S(1)} %add_add_fusion.3), channel_id=1, source_target_pairs={{0,3},{1,2},{2,1},{3,0},{4,7},{5,6},{6,5},{7,4},{8,11},{9,10},{10,... | collective-permute-start | bytes 196616 | tf_op jit(solution)/shard_map/ppermute | solution.py:311
  81.5 7.2 %collective-permute-start.17 = (f32[64,256]{1,0:T(8,128)S(1)}, f32[64,256]{1,0:T(8,128)S(1)}, u32[]{:S(2)}, u32[]{:S(2)}) collective-permute-start(f32[64,256]{1,0:T(8,128)S(1)} %add_add_fusion.3), channel_id=1, source_target_pairs={{0,2},{1,3},{2,0},{3,1},{4,6},{5,7},{6,4},{7,5},{8,10},{9,11},{10,... | collective-permute-start | bytes 196616 | tf_op jit(solution)/shard_map/ppermute | solution.py:311
  81.7 8.2 %collective-permute-start.16 = (f32[64,256]{1,0:T(8,128)S(1)}, f32[64,256]{1,0:T(8,128)S(1)}, u32[]{:S(2)}, u32[]{:S(2)}) collective-permute-start(f32[64,256]{1,0:T(8,128)S(1)} %add_add_fusion.3), channel_id=1, source_target_pairs={{0,1},{1,0},{2,3},{3,2},{4,5},{5,4},{6,7},{7,6},{8,9},{9,8},{10,11... | collective-permute-start | bytes 196616 | tf_op jit(solution)/shard_map/ppermute | solution.py:311
  82.3 31.0 %collective-permute-start.10 = (f32[5,256,128]{2,1,0:T(8,128)S(1)}, f32[5,256,128]{2,1,0:T(8,128)S(1)}, u32[]{:S(2)}, u32[]{:S(2)}) collective-permute-start(f32[5,256,128]{2,1,0:T(8,128)S(1)} %get-tuple-element.42), channel_id=1, source_target_pairs={{0,4},{4,8},{8,12},{12,16},{16,20},{20,24},{24,28},{1,5},{5,9},{9,... | collective-permute-start | bytes 1966088 | tf_op jit(solution)/shard_map/ppermute | solution.py:18
  83.6 29.6 %collective-permute-start.11 = (f32[5,256,128]{2,1,0:T(8,128)S(1)}, f32[5,256,128]{2,1,0:T(8,128)S(1)}, u32[]{:S(2)}, u32[]{:S(2)}) collective-permute-start(f32[5,256,128]{2,1,0:T(8,128)S(1)} %get-tuple-element.43), channel_id=1, source_target_pairs={{4,0},{8,4},{12,8},{16,12},{20,16},{24,20},{28,24},{5,1},{9,5},{13... | collective-permute-start | bytes 1966088 | tf_op jit(solution)/shard_map/ppermute | solution.py:18
  85.1 28.2 %collective-permute-start.6 = (f32[2,640,128]{2,1,0:T(8,128)S(1)}, f32[2,640,128]{2,1,0:T(8,128)S(1)}, u32[]{:S(2)}, u32[]{:S(2)}) collective-permute-start(f32[2,640,128]{2,1,0:T(8,128)S(1)} %get-tuple-element.38), channel_id=1, source_target_pairs={{0,1},{1,2},{2,3},{4,5},{5,6},{6,7},{8,9},{9,10},{10,11},{12,13},{... | collective-permute-start | bytes 1966088 | tf_op jit(solution)/shard_map/ppermute | solution.py:18
  88.7 24.6 %collective-permute-start.7 = (f32[2,640,128]{2,1,0:T(8,128)S(1)}, f32[2,640,128]{2,1,0:T(8,128)S(1)}, u32[]{:S(2)}, u32[]{:S(2)}) collective-permute-start(f32[2,640,128]{2,1,0:T(8,128)S(1)} %get-tuple-element.39), channel_id=1, source_target_pairs={{1,0},{2,1},{3,2},{5,4},{6,5},{7,6},{9,8},{10,9},{11,10},{13,12},{... | collective-permute-start | bytes 1966088 | tf_op jit(solution)/shard_map/ppermute | solution.py:18
  90.0 10.3 %collective-permute-start.21 = (f32[64,256]{1,0:T(8,128)S(1)}, f32[64,256]{1,0:T(8,128)S(1)}, u32[]{:S(2)}, u32[]{:S(2)}) collective-permute-start(f32[64,256]{1,0:T(8,128)S(1)} %add_add_fusion.2), channel_id=1, source_target_pairs={{0,24},{4,28},{8,16},{12,20},{16,8},{20,12},{24,0},{28,4},{1,25},{... | collective-permute-start | bytes 196616 | tf_op jit(solution)/shard_map/ppermute | solution.py:311
  100.3 6.1 %collective-permute-start.20 = (f32[64,256]{1,0:T(8,128)S(1)}, f32[64,256]{1,0:T(8,128)S(1)}, u32[]{:S(2)}, u32[]{:S(2)}) collective-permute-start(f32[64,256]{1,0:T(8,128)S(1)} %add_add_fusion.2), channel_id=1, source_target_pairs={{0,16},{4,20},{8,24},{12,28},{16,0},{20,4},{24,8},{28,12},{1,17},{... | collective-permute-start | bytes 196616 | tf_op jit(solution)/shard_map/ppermute | solution.py:311
  106.4 5.2 %collective-permute-start.19 = (f32[64,256]{1,0:T(8,128)S(1)}, f32[64,256]{1,0:T(8,128)S(1)}, u32[]{:S(2)}, u32[]{:S(2)}) collective-permute-start(f32[64,256]{1,0:T(8,128)S(1)} %add_add_fusion.2), channel_id=1, source_target_pairs={{0,8},{4,12},{8,0},{12,4},{16,24},{20,28},{24,16},{28,20},{1,9},{5... | collective-permute-start | bytes 196616 | tf_op jit(solution)/shard_map/ppermute | solution.py:311
  124.0 19.0 %collective-permute-start.24 = (f32[2,2,256,128]{3,2,1,0:T(8,128)S(1)}, f32[2,2,256,128]{3,2,1,0:T(8,128)S(1)}, u32[]{:S(2)}, u32[]{:S(2)}) collective-permute-start(f32[2,2,256,128]{3,2,1,0:T(8,128)S(1)} %get-tuple-element.53), channel_id=1, source_target_pairs={{0,4},{4,8},{8,12},{12,16},{16,20},{20,24},{24,28},{1,5},{5,9},{9,... | collective-permute-start | bytes 1572872 | tf_op jit(solution)/shard_map/ppermute | solution.py:18
  126.5 9.3 %collective-permute-start.28 = (f32[64,256]{1,0:T(8,128)S(1)}, f32[64,256]{1,0:T(8,128)S(1)}, u32[]{:S(2)}, u32[]{:S(2)}) collective-permute-start(f32[64,256]{1,0:T(8,128)S(1)} %get-tuple-element.59), channel_id=1, source_target_pairs={{0,8},{4,12},{8,0},{12,4},{16,24},{20,28},{24,16},{28,20},{1,9},{5... | collective-permute-start | bytes 196616 | tf_op jit(solution)/shard_map/ppermute | solution.py:311
  131.1 7.4 %collective-permute-start.29 = (f32[64,256]{1,0:T(8,128)S(1)}, f32[64,256]{1,0:T(8,128)S(1)}, u32[]{:S(2)}, u32[]{:S(2)}) collective-permute-start(f32[64,256]{1,0:T(8,128)S(1)} %get-tuple-element.60), channel_id=1, source_target_pairs={{0,16},{4,20},{8,24},{12,28},{16,0},{20,4},{24,8},{28,12},{1,17},{... | collective-permute-start | bytes 196616 | tf_op jit(solution)/shard_map/ppermute | solution.py:311
  131.1 7.4 %collective-permute-start.30 = (f32[64,256]{1,0:T(8,128)S(1)}, f32[64,256]{1,0:T(8,128)S(1)}, u32[]{:S(2)}, u32[]{:S(2)}) collective-permute-start(f32[64,256]{1,0:T(8,128)S(1)} %get-tuple-element.61), channel_id=1, source_target_pairs={{0,24},{4,28},{8,16},{12,20},{16,8},{20,12},{24,0},{28,4},{1,25},{... | collective-permute-start | bytes 196616 | tf_op jit(solution)/shard_map/ppermute | solution.py:311
  132.6 31.2 %collective-permute-start.23 = (f32[2,3,256,128]{3,2,1,0:T(8,128)S(1)}, f32[2,3,256,128]{3,2,1,0:T(8,128)S(1)}, u32[]{:S(2)}, u32[]{:S(2)}) collective-permute-start(f32[2,3,256,128]{3,2,1,0:T(8,128)S(1)} %get-tuple-element.52), channel_id=1, source_target_pairs={{0,4},{4,8},{8,12},{12,16},{16,20},{20,24},{24,28},{1,5},{5,9},{9,... | collective-permute-start | bytes 2359304 | tf_op jit(solution)/shard_map/ppermute | solution.py:18
  138.5 7.1 %collective-permute-start.33 = (f32[64,256]{1,0:T(8,128)S(1)}, f32[64,256]{1,0:T(8,128)S(1)}, u32[]{:S(2)}, u32[]{:S(2)}) collective-permute-start(f32[64,256]{1,0:T(8,128)S(1)} %add_add_fusion.1), channel_id=1, source_target_pairs={{0,3},{1,2},{2,1},{3,0},{4,7},{5,6},{6,5},{7,4},{8,11},{9,10},{10,... | collective-permute-start | bytes 196616 | tf_op jit(solution)/shard_map/ppermute | solution.py:311
  138.9 9.5 %collective-permute-start.32 = (f32[64,256]{1,0:T(8,128)S(1)}, f32[64,256]{1,0:T(8,128)S(1)}, u32[]{:S(2)}, u32[]{:S(2)}) collective-permute-start(f32[64,256]{1,0:T(8,128)S(1)} %add_add_fusion.1), channel_id=1, source_target_pairs={{0,2},{1,3},{2,0},{3,1},{4,6},{5,7},{6,4},{7,5},{8,10},{9,11},{10,... | collective-permute-start | bytes 196616 | tf_op jit(solution)/shard_map/ppermute | solution.py:311
  141.7 6.8 %collective-permute-start.31 = (f32[64,256]{1,0:T(8,128)S(1)}, f32[64,256]{1,0:T(8,128)S(1)}, u32[]{:S(2)}, u32[]{:S(2)}) collective-permute-start(f32[64,256]{1,0:T(8,128)S(1)} %add_add_fusion.1), channel_id=1, source_target_pairs={{0,1},{1,0},{2,3},{3,2},{4,5},{5,4},{6,7},{7,6},{8,9},{9,8},{10,11... | collective-permute-start | bytes 196616 | tf_op jit(solution)/shard_map/ppermute | solution.py:311
  143.1 20.7 %collective-permute-start.25 = (f32[2,2,256,128]{3,2,1,0:T(8,128)S(1)}, f32[2,2,256,128]{3,2,1,0:T(8,128)S(1)}, u32[]{:S(2)}, u32[]{:S(2)}) collective-permute-start(f32[2,2,256,128]{3,2,1,0:T(8,128)S(1)} %shard_map.101), channel_id=1, source_target_pairs={{0,1},{1,2},{2,3},{4,5},{5,6},{6,7},{8,9},{9,10},{10,11},{12,13},{... | collective-permute-start | bytes 1572872 | tf_op jit(solution)/shard_map/ppermute | solution.py:18
  148.5 5.2 %collective-permute-start.36 = (f32[64,256]{1,0:T(8,128)S(1)}, f32[64,256]{1,0:T(8,128)S(1)}, u32[]{:S(2)}, u32[]{:S(2)}) collective-permute-start(f32[64,256]{1,0:T(8,128)S(1)} %add_add_fusion), channel_id=1, source_target_pairs={{0,24},{4,28},{8,16},{12,20},{16,8},{20,12},{24,0},{28,4},{1,25},{... | collective-permute-start | bytes 196616 | tf_op jit(solution)/shard_map/ppermute | solution.py:311
  149.0 5.9 %collective-permute-start.35 = (f32[64,256]{1,0:T(8,128)S(1)}, f32[64,256]{1,0:T(8,128)S(1)}, u32[]{:S(2)}, u32[]{:S(2)}) collective-permute-start(f32[64,256]{1,0:T(8,128)S(1)} %add_add_fusion), channel_id=1, source_target_pairs={{0,16},{4,20},{8,24},{12,28},{16,0},{20,4},{24,8},{28,12},{1,17},{... | collective-permute-start | bytes 196616 | tf_op jit(solution)/shard_map/ppermute | solution.py:311
  156.0 7.8 %collective-permute-start.26 = (f32[2,2,128,128]{3,2,1,0:T(8,128)S(1)}, f32[2,2,128,128]{3,2,1,0:T(8,128)S(1)}, u32[]{:S(2)}, u32[]{:S(2)}) collective-permute-start(f32[2,2,128,128]{3,2,1,0:T(8,128)S(1)} %get-tuple-element.54), channel_id=1, source_target_pairs={{0,1},{1,2},{2,3},{4,5},{5,6},{6,7},{8,9},{9,10},{10,11},{12,13},{... | collective-permute-start | bytes 786440 | tf_op jit(solution)/shard_map/ppermute | solution.py:18
  (13 other events, 70.4 us)
where the time goes:
time: 166 us; the launch traced here: 165 us
  starting transfers between devices  70.3 us (42%)
  waiting for transfers between devices  62.2 us (37%)
  Pallas kernels  23.6 us (14%)
  local copies, waits for them, and re-layouts  6.41 us (4%)
  between operations  2.35 us (1%)
    ppermute x22, waiting for transfers between devices, swap(): lax.ppermute(value, axis, [(source, source ^ mask) for source in range(co...  41.5 us
    ppermute x22, starting transfers between devices, swap(): lax.ppermute(value, axis, [(source, source ^ mask) for source in range(co...  37 us
    ppermute x16, starting transfers between devices, shift(): lax.ppermute(value, axis, [(source, source + steps) for source in range(l...  33.3 us
    pallas_call x10, Pallas kernels, vmem_call(): pl.pallas_call(kernel, in_specs=smem + [vmem] * len(operands), out_specs=...  23.6 us
    ppermute x16, waiting for transfers between devices, shift(): lax.ppermute(value, axis, [(source, source + steps) for source in range(l...  20.7 us
  transfers between devices with their start and end apart: 38, of which 16 were waited for; matrix products, arithmetic and copies ran while one was open for 2% of the time, Pallas kernels for 4%

commit v1 on v0

--- a/solution.py
+++ b/solution.py
@@ -73,10 +73,8 @@
     me, met, mo, mot, le, let, lo, lot = (tab_ref.at[i] for i in range(8))
 
     def left(high_table, low_table, high, low):
-        return dot(high_table[...], high) + dot(high_table[...], low) + dot(low_table[...], high)
-
-    def right(high, low, high_table, low_table):
-        return dot(high, high_table[...]) + dot(low, high_table[...]) + dot(high, low_table[...])
+        both_tables = dot(jnp.concatenate([high_table[...], low_table[...]], axis=0), high)
+        return both_tables[:length] + both_tables[length:] + dot(high_table[...], low)
 
     def pair(step, carry):
         first_slot = start + 2 * step
@@ -125,31 +123,37 @@
                 residue = residue * alive
             return split(jnp.concatenate([residue * r, residue * i], axis=1))
 
-        def middle(even, odd, f):
-            eu, ev = fold(even)
-            ou, ov = fold(odd)
-            uh, ul = split(jnp.concatenate([eu, ou], axis=0))
-            vh, vl = split(jnp.concatenate([ev, ov], axis=0))
-            wave_even = right(uh, ul, met, let)
-            wave_odd = right(vh, vl, mot, lot)
-            eh, el = weigh(wave_even, sorted_ref[slots[f], :, :LANES], f)
-            oh, ol = weigh(wave_odd, sorted_ref[slots[f], :, LANES:], f)
-            e = right(eh, el, me, le)
-            o = right(oh, ol, mo, lo)
-            near, far = e + o, e - o
-
-            def rejoin(at):
-                return split(
-                    jnp.concatenate(
-                        [
-                            jnp.concatenate([near[at, :LANES], far[at, :LANES]], axis=1),
-                            jnp.concatenate([near[at, LANES:], far[at, LANES:]], axis=1),
-                        ],
-                        axis=0,
-                    )
-                )
-
-            return rejoin(slice(0, half)) + rejoin(slice(half, length))
+        def stacked(pairs, high_table, low_table):
+            highs = [pair[0] for pair in pairs]
+            size = length * len(highs)
+            big = dot(jnp.concatenate(highs + [pair[1] for pair in pairs], axis=0), high_table[...])
+            small = dot(jnp.concatenate(highs, axis=0), low_table[...])
+            total = big[:size] + big[size:] + small
+            return [total[f * length : (f + 1) * length] for f in both]
+
+        def middle(halves):
+            us, vs = [], []
+            for even, odd in halves:
+                eu, ev = fold(even)
+                ou, ov = fold(odd)
+                us.append(split(jnp.concatenate([eu, ou], axis=0)))
+                vs.append(split(jnp.concatenate([ev, ov], axis=0)))
+            wave_even = stacked(us, met, let)
+            wave_odd = stacked(vs, mot, lot)
+            es = [weigh(wave_even[f], sorted_ref[slots[f], :, :LANES], f) for f in both]
+            os = [weigh(wave_odd[f], sorted_ref[slots[f], :, LANES:], f) for f in both]
+            back_even = stacked(es, me, le)
+            back_odd = stacked(os, mo, lo)
+            results = []
+            for e, o in zip(back_even, back_odd):
+                near, far = e + o, e - o
+                pieces = ()
+                for at in (slice(0, half), slice(half, length)):
+                    top = jnp.concatenate([near[at, :LANES], far[at, :LANES]], axis=1)
+                    low = jnp.concatenate([near[at, LANES:], far[at, LANES:]], axis=1)
+                    pieces += split(jnp.concatenate([top, low], axis=0))
+                results.append(pieces)
+            return results
 
         def exit_terms(f, e, o):
             mask = lane[:half] >= turn[f]
@@ -173,7 +177,7 @@
 
         entered = [enter(f) for f in both]
         halves = [(left(me, le, uh, ul), left(mo, lo, vh, vl)) for uh, ul, vh, vl in entered]
-        joined = [middle(even, odd, f) for f, (even, odd) in zip(both, halves)]
+        joined = middle(halves)
         ends = [(left(met, let, eh, el), left(mot, lot, oh, ol)) for eh, el, oh, ol in joined]
         for f, (e, o) in zip(both, ends):
             exit_terms(f, e, o)

time: 166 us -> 165 us (level)
  no operation moved by 1% of the time
where the time goes in v1:
time: 165 us
  starting transfers between devices  70.3 us (43%)
  waiting for transfers between devices  62.2 us (38%)
  Pallas kernels  23.2 us (14%)
  local copies, waits for them, and re-layouts  6.41 us (4%)
  between operations  2.35 us (1%)
    ppermute x22, waiting for transfers between devices, swap(): lax.ppermute(value, axis, [(source, source ^ mask) for source in range(co...  41.5 us
    ppermute x22, starting transfers between devices, swap(): lax.ppermute(value, axis, [(source, source ^ mask) for source in range(co...  37 us
    ppermute x16, starting transfers between devices, shift(): lax.ppermute(value, axis, [(source, source + steps) for source in range(l...  33.2 us
    pallas_call x10, Pallas kernels, vmem_call(): pl.pallas_call(kernel, in_specs=smem + [vmem] * len(operands), out_specs=...  23.2 us
    ppermute x16, waiting for transfers between devices, shift(): lax.ppermute(value, axis, [(source, source + steps) for source in range(l...  20.7 us
  transfers between devices with their start and end apart: 38, of which 16 were waited for; matrix products, arithmetic and copies ran while one was open for 2% of the time, Pallas kernels for 4%

profile of v1, /device:TPU:0, one launch (start us, length us, event | category | flops | bytes accessed | tf_op | source)
XLA Modules:
  0.0 164.5 jit_solution(7386200312748323873)
XLA Ops:
  3.2 2.1 %slice.11 = f32[2,256,384]{2,1,0:T(8,128)} slice(f32[2,384,384]{2,1,0:T(8,128)} %refs_6_.1), slice={[0:2], [0:256], [0:384]} | slice | bytes 1572864 | tf_op jit(solution)/shard_map/slice | solution.py:397
  7.3 5.4 %shard_map.95.refs_5_ = f32[8,256,256]{2,1,0:T(8,128)S(1)} custom-call(s32[1,1]{1,0:T(1,128)S(6)} %copy.12.count_ref.refs_0_, bf16[256,256]{1,0:T(8,128)(2,1)S(1)} %copy-done.5, bf16[256,256]{1,0:T(8,128)(2,1)S(1)} %copy-done.4, f32[8,256,256]{2,1,0:T(8,128)S(1)} %bitcast.2), custom_call_target="tpu_custom_call" | custom-call | tf_op jit(solution)/shard_map/pallas_call | solution.py:303
  12.7 6.2 %collective-permute-done.refs_7_ = f32[2,256,256]{2,1,0:T(8,128)} collective-permute-done((f32[2,256,256]{2,1,0:T(8,128)S(1)}, f32[2,256,256]{2,1,0:T(8,128)}, u32[]{:S(2)}, u32[]{:S(2)}) %collective-permute-start) | collective-permute-done | bytes 524320 | tf_op jit(solution)/shard_map/ppermute | solution.py:18
  22.9 9.1 %collective-permute-done.1.refs_8_ = f32[2,128,256]{2,1,0:T(8,128)S(1)} collective-permute-done((f32[2,128,256]{2,1,0:T(8,128)}, f32[2,128,256]{2,1,0:T(8,128)S(1)}, u32[]{:S(2)}, u32[]{:S(2)}) %collective-permute-start.1) | collective-permute-done | bytes 262176 | tf_op jit(solution)/shard_map/ppermute | solution.py:18
  34.3 5.0 %shard_map.96 = (f32[2,5,640,128]{3,2,1,0:T(8,128)S(1)}, f32[2,5,640,128]{3,2,1,0:T(8,128)S(1)}, f32[5,256,128]{2,1,0:T(8,128)S(1)}, f32[5,256,128]{2,1,0:T(8,12...) custom-call(s32[1,1]{1,0:T(1,128)S(6)} %copy.12.count_ref.refs_0_, ...), custom_call_target="tpu_custom_call" | custom-call | tf_op jit(solution)/shard_map/pallas_call | solution.py:303
  39.5 6.3 %collective-permute-start.8 = (f32[2,640,128]{2,1,0:T(8,128)S(1)}, f32[2,640,128]{2,1,0:T(8,128)S(1)}, u32[]{:S(2)}, u32[]{:S(2)}) collective-permute-start(f32[2,640,128]{2,1,0:T(8,128)S(1)} %get-tuple-element.40), channel_id=1, source_target_pairs={{0,1},{1,2},{2,3},{4,5},{5,6},{6,7},{8,9},{9,10},{10,11},{12,13},{... | collective-permute-start | bytes 1966088 | tf_op jit(solution)/shard_map/ppermute | solution.py:18
  47.1 2.1 %collective-permute-start.4 = (f32[5,256,128]{2,1,0:T(8,128)S(1)}, f32[5,256,128]{2,1,0:T(8,128)S(1)}, u32[]{:S(2)}, u32[]{:S(2)}) collective-permute-start(f32[5,256,128]{2,1,0:T(8,128)S(1)} %get-tuple-element.36), channel_id=1, source_target_pairs={{0,4},{4,8},{8,12},{12,16},{16,20},{20,24},{24,28},{1,5},{5,9},{9,... | collective-permute-start | bytes 1966088 | tf_op jit(solution)/shard_map/ppermute | solution.py:18
  50.6 4.2 %collective-permute-start.13 = (f32[64,256]{1,0:T(8,128)S(1)}, f32[64,256]{1,0:T(8,128)S(1)}, u32[]{:S(2)}, u32[]{:S(2)}) collective-permute-start(f32[64,256]{1,0:T(8,128)S(1)} %get-tuple-element.47), channel_id=1, source_target_pairs={{0,8},{4,12},{8,0},{12,4},{16,24},{20,28},{24,16},{28,20},{1,9},{5... | collective-permute-start | bytes 196616 | tf_op jit(solution)/shard_map/ppermute | solution.py:315
  54.8 12.7 %collective-permute-done.13 = f32[64,256]{1,0:T(8,128)S(1)} collective-permute-done((f32[64,256]{1,0:T(8,128)S(1)}, f32[64,256]{1,0:T(8,128)S(1)}, u32[]{:S(2)}, u32[]{:S(2)}) %collective-permute-start.13) | collective-permute-done | bytes 65568 | tf_op jit(solution)/shard_map/ppermute | solution.py:315
  67.5 4.3 %collective-permute-done.14 = f32[64,256]{1,0:T(8,128)S(1)} collective-permute-done((f32[64,256]{1,0:T(8,128)S(1)}, f32[64,256]{1,0:T(8,128)S(1)}, u32[]{:S(2)}, u32[]{:S(2)}) %collective-permute-start.14) | collective-permute-done | bytes 65568 | tf_op jit(solution)/shard_map/ppermute | solution.py:315
  72.0 4.9 %collective-permute-done.15 = f32[64,256]{1,0:T(8,128)S(1)} collective-permute-done((f32[64,256]{1,0:T(8,128)S(1)}, f32[64,256]{1,0:T(8,128)S(1)}, u32[]{:S(2)}, u32[]{:S(2)}) %collective-permute-start.15) | collective-permute-done | bytes 65568 | tf_op jit(solution)/shard_map/ppermute | solution.py:315
  77.0 4.3 %collective-permute-start.18 = (f32[64,256]{1,0:T(8,128)S(1)}, f32[64,256]{1,0:T(8,128)S(1)}, u32[]{:S(2)}, u32[]{:S(2)}) collective-permute-start(f32[64,256]{1,0:T(8,128)S(1)} %add_add_fusion.3), channel_id=1, source_target_pairs={{0,3},{1,2},{2,1},{3,0},{4,7},{5,6},{6,5},{7,4},{8,11},{9,10},{10,... | collective-permute-start | bytes 196616 | tf_op jit(solution)/shard_map/ppermute | solution.py:315
  84.9 3.6 %collective-permute-start.6 = (f32[2,640,128]{2,1,0:T(8,128)S(1)}, f32[2,640,128]{2,1,0:T(8,128)S(1)}, u32[]{:S(2)}, u32[]{:S(2)}) collective-permute-start(f32[2,640,128]{2,1,0:T(8,128)S(1)} %get-tuple-element.38), channel_id=1, source_target_pairs={{0,1},{1,2},{2,3},{4,5},{5,6},{6,7},{8,9},{9,10},{10,11},{12,13},{... | collective-permute-start | bytes 1966088 | tf_op jit(solution)/shard_map/ppermute | solution.py:18
  89.8 5.7 %collective-permute-start.21 = (f32[64,256]{1,0:T(8,128)S(1)}, f32[64,256]{1,0:T(8,128)S(1)}, u32[]{:S(2)}, u32[]{:S(2)}) collective-permute-start(f32[64,256]{1,0:T(8,128)S(1)} %add_add_fusion.2), channel_id=1, source_target_pairs={{0,24},{4,28},{8,16},{12,20},{16,8},{20,12},{24,0},{28,4},{1,25},{... | collective-permute-start | bytes 196616 | tf_op jit(solution)/shard_map/ppermute | solution.py:315
  95.6 4.5 %collective-permute-done.21 = f32[64,256]{1,0:T(8,128)S(1)} collective-permute-done((f32[64,256]{1,0:T(8,128)S(1)}, f32[64,256]{1,0:T(8,128)S(1)}, u32[]{:S(2)}, u32[]{:S(2)}) %collective-permute-start.21) | collective-permute-done | bytes 65568 | tf_op jit(solution)/shard_map/ppermute | solution.py:315
  100.1 3.8 %collective-permute-start.20 = (f32[64,256]{1,0:T(8,128)S(1)}, f32[64,256]{1,0:T(8,128)S(1)}, u32[]{:S(2)}, u32[]{:S(2)}) collective-permute-start(f32[64,256]{1,0:T(8,128)S(1)} %add_add_fusion.2), channel_id=1, source_target_pairs={{0,16},{4,20},{8,24},{12,28},{16,0},{20,4},{24,8},{28,12},{1,17},{... | collective-permute-start | bytes 196616 | tf_op jit(solution)/shard_map/ppermute | solution.py:315
  103.9 2.2 %collective-permute-done.20 = f32[64,256]{1,0:T(8,128)S(1)} collective-permute-done((f32[64,256]{1,0:T(8,128)S(1)}, f32[64,256]{1,0:T(8,128)S(1)}, u32[]{:S(2)}, u32[]{:S(2)}) %collective-permute-start.20) | collective-permute-done | bytes 65568 | tf_op jit(solution)/shard_map/ppermute | solution.py:315
  106.2 3.0 %collective-permute-start.19 = (f32[64,256]{1,0:T(8,128)S(1)}, f32[64,256]{1,0:T(8,128)S(1)}, u32[]{:S(2)}, u32[]{:S(2)}) collective-permute-start(f32[64,256]{1,0:T(8,128)S(1)} %add_add_fusion.2), channel_id=1, source_target_pairs={{0,8},{4,12},{8,0},{12,4},{16,24},{20,28},{24,16},{28,20},{1,9},{5... | collective-permute-start | bytes 196616 | tf_op jit(solution)/shard_map/ppermute | solution.py:315
  109.2 2.2 %collective-permute-done.19 = f32[64,256]{1,0:T(8,128)S(1)} collective-permute-done((f32[64,256]{1,0:T(8,128)S(1)}, f32[64,256]{1,0:T(8,128)S(1)}, u32[]{:S(2)}, u32[]{:S(2)}) %collective-permute-start.19) | collective-permute-done | bytes 65568 | tf_op jit(solution)/shard_map/ppermute | solution.py:315
  111.5 1.5 collective-permute-done.22.refs_17_
  113.1 10.3 %shard_map.100 = (f32[2,5,640,128]{3,2,1,0:T(8,128)S(1)}, f32[2,384,384]{2,1,0:T(8,128)S(1)}, f32[2,256,256]{2,1,0:T(8,128)S(1)}, f32[2,2,256,128]{3,2,1,0:T(8,1...) custom-call(s32[1,1]{1,0:T(1,128)S(6)} %copy.12.count_ref.refs_0_, ...), custom_call_target="tpu_custom_call" | custom-call | tf_op jit(solution)/shard_map/pallas_call | solution.py:303
  123.5 2.4 %collective-permute-start.24 = (f32[2,2,256,128]{3,2,1,0:T(8,128)S(1)}, f32[2,2,256,128]{3,2,1,0:T(8,128)S(1)}, u32[]{:S(2)}, u32[]{:S(2)}) collective-permute-start(f32[2,2,256,128]{3,2,1,0:T(8,128)S(1)} %get-tuple-element.53), channel_id=1, source_target_pairs={{0,4},{4,8},{8,12},{12,16},{16,20},{20,24},{24,28},{1,5},{5,9},{9,... | collective-permute-start | bytes 1572872 | tf_op jit(solution)/shard_map/ppermute | solution.py:18
  126.0 4.6 %collective-permute-start.28 = (f32[64,256]{1,0:T(8,128)S(1)}, f32[64,256]{1,0:T(8,128)S(1)}, u32[]{:S(2)}, u32[]{:S(2)}) collective-permute-start(f32[64,256]{1,0:T(8,128)S(1)} %get-tuple-element.59), channel_id=1, source_target_pairs={{0,8},{4,12},{8,0},{12,4},{16,24},{20,28},{24,16},{28,20},{1,9},{5... | collective-permute-start | bytes 196616 | tf_op jit(solution)/shard_map/ppermute | solution.py:315
  130.5 1.5 collective-permute-start.30
  132.1 3.1 %collective-permute-start.23 = (f32[2,3,256,128]{3,2,1,0:T(8,128)S(1)}, f32[2,3,256,128]{3,2,1,0:T(8,128)S(1)}, u32[]{:S(2)}, u32[]{:S(2)}) collective-permute-start(f32[2,3,256,128]{3,2,1,0:T(8,128)S(1)} %get-tuple-element.52), channel_id=1, source_target_pairs={{0,4},{4,8},{8,12},{12,16},{16,20},{20,24},{24,28},{1,5},{5,9},{9,... | collective-permute-start | bytes 2359304 | tf_op jit(solution)/shard_map/ppermute | solution.py:18
  135.2 2.8 %collective-permute-done.29 = f32[64,256]{1,0:T(8,128)S(1)} collective-permute-done((f32[64,256]{1,0:T(8,128)S(1)}, f32[64,256]{1,0:T(8,128)S(1)}, u32[]{:S(2)}, u32[]{:S(2)}) %collective-permute-start.29) | collective-permute-done | bytes 65568 | tf_op jit(solution)/shard_map/ppermute | solution.py:315
  138.4 2.7 %collective-permute-start.32 = (f32[64,256]{1,0:T(8,128)S(1)}, f32[64,256]{1,0:T(8,128)S(1)}, u32[]{:S(2)}, u32[]{:S(2)}) collective-permute-start(f32[64,256]{1,0:T(8,128)S(1)} %add_add_fusion.1), channel_id=1, source_target_pairs={{0,2},{1,3},{2,0},{3,1},{4,6},{5,7},{6,4},{7,5},{8,10},{9,11},{10,... | collective-permute-start | bytes 196616 | tf_op jit(solution)/shard_map/ppermute | solution.py:315
  142.5 2.6 %collective-permute-start.25 = (f32[2,2,256,128]{3,2,1,0:T(8,128)S(1)}, f32[2,2,256,128]{3,2,1,0:T(8,128)S(1)}, u32[]{:S(2)}, u32[]{:S(2)}) collective-permute-start(f32[2,2,256,128]{3,2,1,0:T(8,128)S(1)} %shard_map.101), channel_id=1, source_target_pairs={{0,1},{1,2},{2,3},{4,5},{5,6},{6,7},{8,9},{9,10},{10,11},{12,13},{... | collective-permute-start | bytes 1572872 | tf_op jit(solution)/shard_map/ppermute | solution.py:18
  145.2 2.7 %collective-permute-done.32 = f32[64,256]{1,0:T(8,128)S(1)} collective-permute-done((f32[64,256]{1,0:T(8,128)S(1)}, f32[64,256]{1,0:T(8,128)S(1)}, u32[]{:S(2)}, u32[]{:S(2)}) %collective-permute-start.32) | collective-permute-done | bytes 65568 | tf_op jit(solution)/shard_map/ppermute | solution.py:315
  148.5 2.2 %collective-permute-start.35 = (f32[64,256]{1,0:T(8,128)S(1)}, f32[64,256]{1,0:T(8,128)S(1)}, u32[]{:S(2)}, u32[]{:S(2)}) collective-permute-start(f32[64,256]{1,0:T(8,128)S(1)} %add_add_fusion), channel_id=1, source_target_pairs={{0,16},{4,20},{8,24},{12,28},{16,0},{20,4},{24,8},{28,12},{1,17},{... | collective-permute-start | bytes 196616 | tf_op jit(solution)/shard_map/ppermute | solution.py:315
  150.7 1.4 collective-permute-start.34
  157.9 5.4 %collective-permute-done.26.before_low = f32[2,2,128,128]{3,2,1,0:T(8,128)S(1)} collective-permute-done((f32[2,2,128,128]{3,2,1,0:T(8,128)S(1)}, f32[2,2,128,128]{3,2,1,0:T(8,128)S(1)}, u32[]{:S(2)}, u32[]{:S(2)}) %collective-permute-start.26) | collective-permute-done | bytes 262176 | tf_op jit(solution)/shard_map/ppermute | solution.py:18
  (78 shorter events, 27.0 us)
Async XLA Ops:
  1.9 17.0 %collective-permute-start = (f32[2,256,256]{2,1,0:T(8,128)S(1)}, f32[2,256,256]{2,1,0:T(8,128)}, u32[]{:S(2)}, u32[]{:S(2)}) collective-permute-start(f32[2,256,256]{2,1,0:T(8,128)S(1)} %slice.9), channel_id=1, source_target_pairs={{1,0},{2,1},{3,2},{5,4},{6,5},{7,6},{9,8},{10,9},{11,10},{13,12},{... | collective-permute-start | bytes 1572872 | tf_op jit(solution)/shard_map/ppermute | solution.py:18
  5.3 26.8 %collective-permute-start.2 = (f32[2,256,384]{2,1,0:T(8,128)}, f32[2,256,384]{2,1,0:T(8,128)}, u32[]{:S(2)}, u32[]{:S(2)}) collective-permute-start(f32[2,256,384]{2,1,0:T(8,128)} %slice.11), channel_id=1, source_target_pairs={{4,0},{8,4},{12,8},{16,12},{20,16},{24,20},{28,24},{5,1},{9,5},{13... | collective-permute-start | bytes 2359304 | tf_op jit(solution)/shard_map/ppermute | solution.py:18
  18.9 13.1 %collective-permute-start.3 = (f32[2,256,256]{2,1,0:T(8,128)}, f32[2,256,256]{2,1,0:T(8,128)}, u32[]{:S(2)}, u32[]{:S(2)}) collective-permute-start(f32[2,256,256]{2,1,0:T(8,128)} %collective-permute-done.refs_7_), channel_id=1, source_target_pairs={{4,0},{8,4},{12,8},{16,12},{20,16},{24,20},{28,24},{5,1},{9,5},{13... | collective-permute-start | bytes 1572872 | tf_op jit(solution)/shard_map/ppermute | solution.py:18
  20.9 11.1 %collective-permute-start.1 = (f32[2,128,256]{2,1,0:T(8,128)}, f32[2,128,256]{2,1,0:T(8,128)S(1)}, u32[]{:S(2)}, u32[]{:S(2)}) collective-permute-start(f32[2,128,256]{2,1,0:T(8,128)} %slice.10), channel_id=1, source_target_pairs={{1,0},{2,1},{3,2},{5,4},{6,5},{7,6},{9,8},{10,9},{11,10},{13,12},{... | collective-permute-start | bytes 786440 | tf_op jit(solution)/shard_map/ppermute | solution.py:18
  39.3 11.3 %collective-permute-start.12 = (f32[256,256]{1,0:T(8,128)S(1)}, f32[256,256]{1,0:T(8,128)S(1)}, u32[]{:S(2)}, u32[]{:S(2)}) collective-permute-start(f32[256,256]{1,0:T(8,128)S(1)} %get-tuple-element.45), channel_id=1, source_target_pairs={{0,4},{4,0},{8,12},{12,8},{16,20},{20,16},{24,28},{28,24},{1,5},{5... | collective-permute-start | bytes 786440 | tf_op jit(solution)/shard_map/ppermute | solution.py:315
  39.5 41.8 %collective-permute-start.8 = (f32[2,640,128]{2,1,0:T(8,128)S(1)}, f32[2,640,128]{2,1,0:T(8,128)S(1)}, u32[]{:S(2)}, u32[]{:S(2)}) collective-permute-start(f32[2,640,128]{2,1,0:T(8,128)S(1)} %get-tuple-element.40), channel_id=1, source_target_pairs={{0,1},{1,2},{2,3},{4,5},{5,6},{6,7},{8,9},{9,10},{10,11},{12,13},{... | collective-permute-start | bytes 1966088 | tf_op jit(solution)/shard_map/ppermute | solution.py:18
  45.8 35.8 %collective-permute-start.9 = (f32[2,640,128]{2,1,0:T(8,128)S(1)}, f32[2,640,128]{2,1,0:T(8,128)S(1)}, u32[]{:S(2)}, u32[]{:S(2)}) collective-permute-start(f32[2,640,128]{2,1,0:T(8,128)S(1)} %get-tuple-element.41), channel_id=1, source_target_pairs={{1,0},{2,1},{3,2},{5,4},{6,5},{7,6},{9,8},{10,9},{11,10},{13,12},{... | collective-permute-start | bytes 1966088 | tf_op jit(solution)/shard_map/ppermute | solution.py:18
  47.1 34.9 %collective-permute-start.4 = (f32[5,256,128]{2,1,0:T(8,128)S(1)}, f32[5,256,128]{2,1,0:T(8,128)S(1)}, u32[]{:S(2)}, u32[]{:S(2)}) collective-permute-start(f32[5,256,128]{2,1,0:T(8,128)S(1)} %get-tuple-element.36), channel_id=1, source_target_pairs={{0,4},{4,8},{8,12},{12,16},{16,20},{20,24},{24,28},{1,5},{5,9},{9,... | collective-permute-start | bytes 1966088 | tf_op jit(solution)/shard_map/ppermute | solution.py:18
  49.3 34.1 %collective-permute-start.5 = (f32[5,256,128]{2,1,0:T(8,128)S(1)}, f32[5,256,128]{2,1,0:T(8,128)S(1)}, u32[]{:S(2)}, u32[]{:S(2)}) collective-permute-start(f32[5,256,128]{2,1,0:T(8,128)S(1)} %get-tuple-element.37), channel_id=1, source_target_pairs={{4,0},{8,4},{12,8},{16,12},{20,16},{24,20},{28,24},{5,1},{9,5},{13... | collective-permute-start | bytes 1966088 | tf_op jit(solution)/shard_map/ppermute | solution.py:18
  50.6 16.9 %collective-permute-start.13 = (f32[64,256]{1,0:T(8,128)S(1)}, f32[64,256]{1,0:T(8,128)S(1)}, u32[]{:S(2)}, u32[]{:S(2)}) collective-permute-start(f32[64,256]{1,0:T(8,128)S(1)} %get-tuple-element.47), channel_id=1, source_target_pairs={{0,8},{4,12},{8,0},{12,4},{16,24},{20,28},{24,16},{28,20},{1,9},{5... | collective-permute-start | bytes 196616 | tf_op jit(solution)/shard_map/ppermute | solution.py:315
  77.0 7.9 %collective-permute-start.18 = (f32[64,256]{1,0:T(8,128)S(1)}, f32[64,256]{1,0:T(8,128)S(1)}, u32[]{:S(2)}, u32[]{:S(2)}) collective-permute-start(f32[64,256]{1,0:T(8,128)S(1)} %add_add_fusion.3), channel_id=1, source_target_pairs={{0,3},{1,2},{2,1},{3,0},{4,7},{5,6},{6,5},{7,4},{8,11},{9,10},{10,... | collective-permute-start | bytes 196616 | tf_op jit(solution)/shard_map/ppermute | solution.py:315
  81.3 7.2 %collective-permute-start.17 = (f32[64,256]{1,0:T(8,128)S(1)}, f32[64,256]{1,0:T(8,128)S(1)}, u32[]{:S(2)}, u32[]{:S(2)}) collective-permute-start(f32[64,256]{1,0:T(8,128)S(1)} %add_add_fusion.3), channel_id=1, source_target_pairs={{0,2},{1,3},{2,0},{3,1},{4,6},{5,7},{6,4},{7,5},{8,10},{9,11},{10,... | collective-permute-start | bytes 196616 | tf_op jit(solution)/shard_map/ppermute | solution.py:315
  81.6 8.2 %collective-permute-start.16 = (f32[64,256]{1,0:T(8,128)S(1)}, f32[64,256]{1,0:T(8,128)S(1)}, u32[]{:S(2)}, u32[]{:S(2)}) collective-permute-start(f32[64,256]{1,0:T(8,128)S(1)} %add_add_fusion.3), channel_id=1, source_target_pairs={{0,1},{1,0},{2,3},{3,2},{4,5},{5,4},{6,7},{7,6},{8,9},{9,8},{10,11... | collective-permute-start | bytes 196616 | tf_op jit(solution)/shard_map/ppermute | solution.py:315
  82.1 31.0 %collective-permute-start.10 = (f32[5,256,128]{2,1,0:T(8,128)S(1)}, f32[5,256,128]{2,1,0:T(8,128)S(1)}, u32[]{:S(2)}, u32[]{:S(2)}) collective-permute-start(f32[5,256,128]{2,1,0:T(8,128)S(1)} %get-tuple-element.42), channel_id=1, source_target_pairs={{0,4},{4,8},{8,12},{12,16},{16,20},{20,24},{24,28},{1,5},{5,9},{9,... | collective-permute-start | bytes 1966088 | tf_op jit(solution)/shard_map/ppermute | solution.py:18
  83.4 29.6 %collective-permute-start.11 = (f32[5,256,128]{2,1,0:T(8,128)S(1)}, f32[5,256,128]{2,1,0:T(8,128)S(1)}, u32[]{:S(2)}, u32[]{:S(2)}) collective-permute-start(f32[5,256,128]{2,1,0:T(8,128)S(1)} %get-tuple-element.43), channel_id=1, source_target_pairs={{4,0},{8,4},{12,8},{16,12},{20,16},{24,20},{28,24},{5,1},{9,5},{13... | collective-permute-start | bytes 1966088 | tf_op jit(solution)/shard_map/ppermute | solution.py:18
  84.9 28.2 %collective-permute-start.6 = (f32[2,640,128]{2,1,0:T(8,128)S(1)}, f32[2,640,128]{2,1,0:T(8,128)S(1)}, u32[]{:S(2)}, u32[]{:S(2)}) collective-permute-start(f32[2,640,128]{2,1,0:T(8,128)S(1)} %get-tuple-element.38), channel_id=1, source_target_pairs={{0,1},{1,2},{2,3},{4,5},{5,6},{6,7},{8,9},{9,10},{10,11},{12,13},{... | collective-permute-start | bytes 1966088 | tf_op jit(solution)/shard_map/ppermute | solution.py:18
  88.5 24.6 %collective-permute-start.7 = (f32[2,640,128]{2,1,0:T(8,128)S(1)}, f32[2,640,128]{2,1,0:T(8,128)S(1)}, u32[]{:S(2)}, u32[]{:S(2)}) collective-permute-start(f32[2,640,128]{2,1,0:T(8,128)S(1)} %get-tuple-element.39), channel_id=1, source_target_pairs={{1,0},{2,1},{3,2},{5,4},{6,5},{7,6},{9,8},{10,9},{11,10},{13,12},{... | collective-permute-start | bytes 1966088 | tf_op jit(solution)/shard_map/ppermute | solution.py:18
  89.8 10.2 %collective-permute-start.21 = (f32[64,256]{1,0:T(8,128)S(1)}, f32[64,256]{1,0:T(8,128)S(1)}, u32[]{:S(2)}, u32[]{:S(2)}) collective-permute-start(f32[64,256]{1,0:T(8,128)S(1)} %add_add_fusion.2), channel_id=1, source_target_pairs={{0,24},{4,28},{8,16},{12,20},{16,8},{20,12},{24,0},{28,4},{1,25},{... | collective-permute-start | bytes 196616 | tf_op jit(solution)/shard_map/ppermute | solution.py:315
  100.1 6.1 %collective-permute-start.20 = (f32[64,256]{1,0:T(8,128)S(1)}, f32[64,256]{1,0:T(8,128)S(1)}, u32[]{:S(2)}, u32[]{:S(2)}) collective-permute-start(f32[64,256]{1,0:T(8,128)S(1)} %add_add_fusion.2), channel_id=1, source_target_pairs={{0,16},{4,20},{8,24},{12,28},{16,0},{20,4},{24,8},{28,12},{1,17},{... | collective-permute-start | bytes 196616 | tf_op jit(solution)/shard_map/ppermute | solution.py:315
  106.2 5.2 %collective-permute-start.19 = (f32[64,256]{1,0:T(8,128)S(1)}, f32[64,256]{1,0:T(8,128)S(1)}, u32[]{:S(2)}, u32[]{:S(2)}) collective-permute-start(f32[64,256]{1,0:T(8,128)S(1)} %add_add_fusion.2), channel_id=1, source_target_pairs={{0,8},{4,12},{8,0},{12,4},{16,24},{20,28},{24,16},{28,20},{1,9},{5... | collective-permute-start | bytes 196616 | tf_op jit(solution)/shard_map/ppermute | solution.py:315
  123.5 19.0 %collective-permute-start.24 = (f32[2,2,256,128]{3,2,1,0:T(8,128)S(1)}, f32[2,2,256,128]{3,2,1,0:T(8,128)S(1)}, u32[]{:S(2)}, u32[]{:S(2)}) collective-permute-start(f32[2,2,256,128]{3,2,1,0:T(8,128)S(1)} %get-tuple-element.53), channel_id=1, source_target_pairs={{0,4},{4,8},{8,12},{12,16},{16,20},{20,24},{24,28},{1,5},{5,9},{9,... | collective-permute-start | bytes 1572872 | tf_op jit(solution)/shard_map/ppermute | solution.py:18
  126.0 9.2 %collective-permute-start.28 = (f32[64,256]{1,0:T(8,128)S(1)}, f32[64,256]{1,0:T(8,128)S(1)}, u32[]{:S(2)}, u32[]{:S(2)}) collective-permute-start(f32[64,256]{1,0:T(8,128)S(1)} %get-tuple-element.59), channel_id=1, source_target_pairs={{0,8},{4,12},{8,0},{12,4},{16,24},{20,28},{24,16},{28,20},{1,9},{5... | collective-permute-start | bytes 196616 | tf_op jit(solution)/shard_map/ppermute | solution.py:315
  130.5 7.4 %collective-permute-start.29 = (f32[64,256]{1,0:T(8,128)S(1)}, f32[64,256]{1,0:T(8,128)S(1)}, u32[]{:S(2)}, u32[]{:S(2)}) collective-permute-start(f32[64,256]{1,0:T(8,128)S(1)} %get-tuple-element.60), channel_id=1, source_target_pairs={{0,16},{4,20},{8,24},{12,28},{16,0},{20,4},{24,8},{28,12},{1,17},{... | collective-permute-start | bytes 196616 | tf_op jit(solution)/shard_map/ppermute | solution.py:315
  130.5 7.4 %collective-permute-start.30 = (f32[64,256]{1,0:T(8,128)S(1)}, f32[64,256]{1,0:T(8,128)S(1)}, u32[]{:S(2)}, u32[]{:S(2)}) collective-permute-start(f32[64,256]{1,0:T(8,128)S(1)} %get-tuple-element.61), channel_id=1, source_target_pairs={{0,24},{4,28},{8,16},{12,20},{16,8},{20,12},{24,0},{28,4},{1,25},{... | collective-permute-start | bytes 196616 | tf_op jit(solution)/shard_map/ppermute | solution.py:315
  132.1 31.2 %collective-permute-start.23 = (f32[2,3,256,128]{3,2,1,0:T(8,128)S(1)}, f32[2,3,256,128]{3,2,1,0:T(8,128)S(1)}, u32[]{:S(2)}, u32[]{:S(2)}) collective-permute-start(f32[2,3,256,128]{3,2,1,0:T(8,128)S(1)} %get-tuple-element.52), channel_id=1, source_target_pairs={{0,4},{4,8},{8,12},{12,16},{16,20},{20,24},{24,28},{1,5},{5,9},{9,... | collective-permute-start | bytes 2359304 | tf_op jit(solution)/shard_map/ppermute | solution.py:18
  138.0 7.2 %collective-permute-start.33 = (f32[64,256]{1,0:T(8,128)S(1)}, f32[64,256]{1,0:T(8,128)S(1)}, u32[]{:S(2)}, u32[]{:S(2)}) collective-permute-start(f32[64,256]{1,0:T(8,128)S(1)} %add_add_fusion.1), channel_id=1, source_target_pairs={{0,3},{1,2},{2,1},{3,0},{4,7},{5,6},{6,5},{7,4},{8,11},{9,10},{10,... | collective-permute-start | bytes 196616 | tf_op jit(solution)/shard_map/ppermute | solution.py:315
  138.4 9.5 %collective-permute-start.32 = (f32[64,256]{1,0:T(8,128)S(1)}, f32[64,256]{1,0:T(8,128)S(1)}, u32[]{:S(2)}, u32[]{:S(2)}) collective-permute-start(f32[64,256]{1,0:T(8,128)S(1)} %add_add_fusion.1), channel_id=1, source_target_pairs={{0,2},{1,3},{2,0},{3,1},{4,6},{5,7},{6,4},{7,5},{8,10},{9,11},{10,... | collective-permute-start | bytes 196616 | tf_op jit(solution)/shard_map/ppermute | solution.py:315
  141.1 6.8 %collective-permute-start.31 = (f32[64,256]{1,0:T(8,128)S(1)}, f32[64,256]{1,0:T(8,128)S(1)}, u32[]{:S(2)}, u32[]{:S(2)}) collective-permute-start(f32[64,256]{1,0:T(8,128)S(1)} %add_add_fusion.1), channel_id=1, source_target_pairs={{0,1},{1,0},{2,3},{3,2},{4,5},{5,4},{6,7},{7,6},{8,9},{9,8},{10,11... | collective-permute-start | bytes 196616 | tf_op jit(solution)/shard_map/ppermute | solution.py:315
  142.5 20.8 %collective-permute-start.25 = (f32[2,2,256,128]{3,2,1,0:T(8,128)S(1)}, f32[2,2,256,128]{3,2,1,0:T(8,128)S(1)}, u32[]{:S(2)}, u32[]{:S(2)}) collective-permute-start(f32[2,2,256,128]{3,2,1,0:T(8,128)S(1)} %shard_map.101), channel_id=1, source_target_pairs={{0,1},{1,2},{2,3},{4,5},{5,6},{6,7},{8,9},{9,10},{10,11},{12,13},{... | collective-permute-start | bytes 1572872 | tf_op jit(solution)/shard_map/ppermute | solution.py:18
  147.9 5.2 %collective-permute-start.36 = (f32[64,256]{1,0:T(8,128)S(1)}, f32[64,256]{1,0:T(8,128)S(1)}, u32[]{:S(2)}, u32[]{:S(2)}) collective-permute-start(f32[64,256]{1,0:T(8,128)S(1)} %add_add_fusion), channel_id=1, source_target_pairs={{0,24},{4,28},{8,16},{12,20},{16,8},{20,12},{24,0},{28,4},{1,25},{... | collective-permute-start | bytes 196616 | tf_op jit(solution)/shard_map/ppermute | solution.py:315
  148.5 6.0 %collective-permute-start.35 = (f32[64,256]{1,0:T(8,128)S(1)}, f32[64,256]{1,0:T(8,128)S(1)}, u32[]{:S(2)}, u32[]{:S(2)}) collective-permute-start(f32[64,256]{1,0:T(8,128)S(1)} %add_add_fusion), channel_id=1, source_target_pairs={{0,16},{4,20},{8,24},{12,28},{16,0},{20,4},{24,8},{28,12},{1,17},{... | collective-permute-start | bytes 196616 | tf_op jit(solution)/shard_map/ppermute | solution.py:315
  155.5 7.8 %collective-permute-start.26 = (f32[2,2,128,128]{3,2,1,0:T(8,128)S(1)}, f32[2,2,128,128]{3,2,1,0:T(8,128)S(1)}, u32[]{:S(2)}, u32[]{:S(2)}) collective-permute-start(f32[2,2,128,128]{3,2,1,0:T(8,128)S(1)} %get-tuple-element.54), channel_id=1, source_target_pairs={{0,1},{1,2},{2,3},{4,5},{5,6},{6,7},{8,9},{9,10},{10,11},{12,13},{... | collective-permute-start | bytes 786440 | tf_op jit(solution)/shard_map/ppermute | solution.py:18
  (13 other events, 70.4 us)
